TPU v7x, 32 devices: a whole 2x2x4 slice. The times are simulated.
32 devices in a mesh: dp: 8 (over z, x), mp: 4 (over y, core).
Axes of the slice: x: 2, y: 2, z: 4, core: 2. Of those that a mesh axis runs over, the one named last changes fastest.
Arguments:
- grad_tiles: bfloat16 [16, 512, 512], P(None, 'dp', 'mp'), may hold values from -8 to 8
- factor_stats: float32 [16, 2, 512, 512], P('dp', None, 'mp'), may hold values from -80 to 500, as said below
- owner_blocks: int32 [8, 2], replicated, may hold values from 0 to 15, as said below
- rotation: int32 [1], replicated, may hold values from 0 to 7
Outputs:
- preconditioned: bfloat16 [16, 512, 512], P(None, 'dp', 'mp')
- new_stats: float32 [16, 2, 512, 512], P('dp', None, 'mp')
Inputs may be any that keep to these rules, and one draw needn't show every extreme that they name: Each matrix factor_stats[slot, side] is symmetric and positive definite. `owner_blocks`: every block number 0 to 15 stands exactly once.
All inputs are finite; a program needn't handle non-finite values.
Results may differ from a plain program's by a relative error of at most 0.0092.
Values may be sent and summed in bfloat16 or wider, within the bound.
No kernel may reach another device: no remote copies, remote signals or barrier semaphores. Data moves between devices by JAX's collectives and lax.ppermute only.
A program may use at most 64 MiB of HBM per device.

v0:
```python
import jax
import jax.numpy as jnp
from jax import lax
from jax.sharding import PartitionSpec as P

ITERS = 2
decay_rate = 0.9
damping = 1.0


def newton_root(factor):
    order = factor.shape[-1]
    identity = jnp.eye(order, dtype=jnp.float32)
    squares = jnp.sum(jnp.square(factor.astype(jnp.float32)), axis=(1, 2), keepdims=True)
    norm_scale = 2.5 / jnp.sqrt(squares)
    moment = (norm_scale * factor.astype(jnp.float32)).astype(jnp.bfloat16)
    current = None
    for newton_step in range(ITERS):
        step_t = ((5.0 * identity - moment.astype(jnp.float32)) * 0.25).astype(jnp.bfloat16)
        if newton_step == 0:
            current = step_t
        else:
            current = jnp.einsum(
                "sij,sjk->sik", current, step_t, preferred_element_type=jnp.float32
            ).astype(jnp.bfloat16)
        if newton_step + 1 < ITERS:
            square = jnp.einsum(
                "sij,sjk->sik", step_t, step_t, preferred_element_type=jnp.float32
            ).astype(jnp.bfloat16)
            partial_m = jnp.einsum(
                "sij,sjk->sik", square, moment, preferred_element_type=jnp.float32
            ).astype(jnp.bfloat16)
            moment = jnp.einsum(
                "sij,sjk->sik", square, partial_m, preferred_element_type=jnp.float32
            ).astype(jnp.bfloat16)
    return current


def body(grad_tiles, factor_stats, owner_blocks, rotation):
    dp_count = lax.axis_size("dp")
    mp_count = lax.axis_size("mp")
    block_count = grad_tiles.shape[0]
    tile_rows = grad_tiles.shape[1]
    tile_cols = grad_tiles.shape[2]
    slots = owner_blocks.shape[1]
    rows_each = factor_stats.shape[2]
    order = factor_stats.shape[3]
    per_slot = mp_count // slots
    part_width = order // per_slot
    my_index = lax.axis_index("mp")
    my_slot = my_index // per_slot
    my_part = my_index % per_slot
    owners = jnp.roll(owner_blocks, rotation[0], axis=0)
    outgoing = jnp.take(grad_tiles, owners.T, axis=0)
    arrived = lax.all_to_all(outgoing, "dp", split_axis=1, concat_axis=1, tiled=True)
    col_part = arrived.reshape(slots, order, tile_cols)
    blocks = lax.all_gather(col_part, "mp", axis=2, tiled=True)
    row_part = lax.dynamic_slice_in_dim(blocks, my_index * rows_each, rows_each, 1)
    left_rows = jnp.einsum("kij,klj->kil", row_part, blocks, preferred_element_type=jnp.float32)
    right_rows = jnp.einsum("kji,kjl->kil", col_part, blocks, preferred_element_type=jnp.float32)
    fresh_rows = jnp.stack([left_rows, right_rows], axis=1)
    new_stats = decay_rate * factor_stats + (1.0 - decay_rate) * fresh_rows
    row_ids = my_index * rows_each + jnp.arange(rows_each)
    identity_rows = (row_ids[:, None] == jnp.arange(order)[None, :]).astype(jnp.float32)
    factor_rows = (new_stats + damping * identity_rows).astype(jnp.bfloat16)
    spread_rows = jnp.repeat(factor_rows, per_slot, axis=0)
    factor = lax.all_to_all(spread_rows, "mp", split_axis=0, concat_axis=2, tiled=True)[0]
    inverse_roots = newton_root(factor)
    grad_block = lax.dynamic_index_in_dim(blocks, my_slot, 0, keepdims=False)
    right_part = lax.dynamic_slice_in_dim(inverse_roots[1], my_part * part_width, part_width, 1)
    right_applied = jnp.dot(grad_block, right_part, preferred_element_type=jnp.float32).astype(
        jnp.bfloat16
    )
    result = jnp.dot(inverse_roots[0], right_applied, preferred_element_type=jnp.float32).astype(
        jnp.bfloat16
    )
    all_parts = lax.all_gather(result, "mp", axis=1, tiled=True)
    slot_parts = all_parts.reshape(order, slots, order)
    grad_squares = jnp.sum(jnp.square(blocks.astype(jnp.float32)), axis=(1, 2))
    result_squares = jnp.sum(jnp.square(slot_parts.astype(jnp.float32)), axis=(0, 2))
    graft_scale = jnp.sqrt(grad_squares) / (jnp.sqrt(result_squares) + 1e-06)
    my_cols = lax.dynamic_slice_in_dim(slot_parts, my_index * tile_cols, tile_cols, 2)
    scaled = (my_cols.astype(jnp.float32) * graft_scale[None, :, None]).astype(jnp.bfloat16)
    outgoing_back = scaled.reshape(dp_count, tile_rows, slots, tile_cols)
    returned = lax.all_to_all(outgoing_back, "dp", split_axis=0, concat_axis=0, tiled=True)
    owner_flat = owners.reshape(-1)
    position = (
        jnp.zeros((block_count,), jnp.int32)
        .at[owner_flat]
        .set(jnp.arange(owner_flat.shape[0], dtype=jnp.int32))
    )
    holder_row = position // slots
    holder_slot = position % slots
    preconditioned = returned[holder_row, :, holder_slot, :]
    return (preconditioned, new_stats)


def solution(mesh):
    return jax.shard_map(
        body,
        mesh=mesh,
        in_specs=(P(None, "dp", "mp"), P("dp", None, "mp", None), P(), P()),
        out_specs=(P(None, "dp", "mp"), P("dp", None, "mp", None)),
        check_vma=False,
    )
```

profile of v0, /device:TPU:0, one launch (start us, length us, event | category | flops | bytes accessed | tf_op | source)
XLA Modules:
  0.0 122.4 jit_solution(869235592168875510)
XLA Ops:
  7.2 0.0 copy-start
  7.2 0.0 all-gather.3.cloned.1.call-start
  7.9 0.8 pad_add_fusion
  8.8 0.1 compare_and_fusion
  8.8 0.1 reshape.116
  8.9 0.6 gather_fusion
  9.5 0.1 broadcast_select_fusion
  9.7 16.0 %all_to_all.19 = bf16[2,8,64,128]{3,2,0,1:T(8,128)(2,1)S(1)} all-to-all(bf16[2,8,64,128]{3,2,0,1:T(8,128)(2,1)S(1)} %copy.41), channel_id=1, replica_groups=mesh['dp'=8,'mp'=4] {'dp'}, dimensions={1} | all-to-all | bytes 524288 | tf_op jit(solution)/shard_map/all_to_all | solution.py:55
  25.7 0.7 copy.42
  26.4 0.0 all-gather.3.cloned.1.call-update
  26.4 0.8 fusion.12
  27.2 15.2 %all-gather.3.cloned.1.call-done = bf16[2,512,512]{2,1,0:T(8,128)(2,1)} async-done(((bf16[2,512,128]{2,1,0:T(8,128)(2,1)}), bf16[2,512,512]{2,1,0:T(8,128)(2,1)}) %all-gather.3.cloned.1.call-update) | async-done | bytes 1048592 | tf_op jit(solution)/shard_map/all_gather | solution.py:57
  42.4 1.7 %convolution_bitcast_fusion = f32[2,1,128,512]{3,2,0,1:T(8,128)S(1)} fusion(bf16[2,512,128]{2,1,0:T(8,128)(2,1)} %bitcast.43, bf16[2,512,512]{2,1,0:T(8,128)(2,1)} %all-gather.3.cloned.1.call-done), kind=kOutput, calls=%fused_computation.15 | convolution fusion | flops 134217728 | bytes 1835008 | tf_op jit(solution)/shard_map/kji,kjl->kil/dot_general | solution.py:60
  44.2 0.5 convolution_bitcast_fusion.1
  44.7 0.3 add_convert_fusion
  45.0 1.1 broadcast_in_dim.32
  46.1 3.5 %all-to-all-start.1 = ((bf16[4,2,128,512]{3,2,1,0:T(8,128)(2,1)}), bf16[4,2,128,512]{3,2,1,0:T(8,128)(2,1)S(1)}, u32[]{:S(2)}, u32[]{:S(2)}) async-start(bf16[4,2,128,512]{3,2,1,0:T(8,128)(2,1)} %bitcast.6), calls=%async_computation.1 | async-start | bytes 2097152 | tf_op jit(solution)/shard_map/all_to_all | solution.py:67
  49.6 0.0 all-gather.5.cloned.1.call-start
  49.7 1.2 fusion.2
  50.9 13.2 %all-to-all-done.1 = bf16[4,2,128,512]{3,2,1,0:T(8,128)(2,1)S(1)} async-done(((bf16[4,2,128,512]{3,2,1,0:T(8,128)(2,1)}), bf16[4,2,128,512]{3,2,1,0:T(8,128)(2,1)S(1)}, u32[]{:S(2)}, u32[]{:S(2)}) %all-to-all-start.1) | async-done | bytes 1048608 | tf_op jit(solution)/shard_map/all_to_all | solution.py:67
  64.0 0.3 convert_bitcast_fusion
  64.3 0.2 copy.45
  64.5 0.4 fusion
  64.9 0.3 multiply_convert_fusion.2
  65.3 1.0 copy-done.4
  66.2 0.0 copy-done.2
  66.2 1.7 %convolution_convert_fusion.3 = bf16[2,512,512]{2,1,0:T(8,128)(2,1)} fusion(bf16[2,512,512]{2,1,0:T(8,128)(2,1)S(1)} %multiply_convert_fusion.2, f32[512,512]{1,0:T(8,128)S(1)} %copy-done.2), kind=kOutput, calls=%fused_computation.14 | convolution fusion | flops 539492352 | bytes 3145728 | tf_op jit(solution)/shard_map/sij,sjk->sik/dot_general | solution.py:27
  67.9 4.2 %multiply_convert_fusion = bf16[2,512,512]{2,1,0:T(8,128)(2,1)} fusion(bf16[2,512,512]{2,1,0:T(8,128)(2,1)} %convolution_convert_fusion.3, bf16[2,512,512]{2,1,0:T(8,128)(2,1)} %copy-done.4, f32[512,512]{1,0:T(8,128)S(1)} %copy-done.3), kind=kOutput, calls=%fused_computation.8 | convolution fusion | flops 1076887552 | bytes 4194304 | tf_op jit(solution)/shard_map/sij,sjk->sik/dot_general | solution.py:33
  72.2 2.3 %convolution_convert_fusion = bf16[2,512,512]{2,1,0:T(8,128)(2,1)S(1)} fusion(bf16[2,512,512]{2,1,0:T(8,128)(2,1)} %multiply_convert_fusion, bf16[2,512,512]{2,1,0:T(8,128)(2,1)} %copy-done.4, f32[512,512]{1,0:T(8,128)S(1)} %copy-done.3), kind=kOutput, calls=%fused_computation.11 | convolution fusion | flops 539492352 | bytes 4194304 | tf_op jit(solution)/shard_map/sij,sjk->sik/dot_general | solution.py:23
  74.4 0.0 copy-start.7
  74.4 1.0 copy-done.7
  75.4 2.5 %convolution_convert_fusion.4 = bf16[512,256]{1,0:T(8,128)(2,1)} fusion(bf16[2,512,512]{2,1,0:T(8,128)(2,1)} %copy-done.7, bf16[2,512,512]{2,1,0:T(8,128)(2,1)S(1)} %copy-done.1, s32[]{:T(128)S(6)} %select_n.76, bf16[1,512,512]{2,1,0:T(8,128)(2,1)S(1)} %slice.13, s32[]{:T(128)S(6)} %select_n.78), kind=kOutput, calls=%fused_computation.17 | convolution fusion | flops 268697600 | bytes 1572872 | tf_op jit(solution)/shard_map/dot_general | solution.py:74
  77.9 0.0 all-gather.5.cloned.1.call-update
  78.0 0.4 multiply_reduce_fusion.1
  78.3 16.6 %all-gather.5.cloned.1.call-done = bf16[512,1024]{1,0:T(8,128)(2,1)} async-done(((bf16[512,256]{1,0:T(8,128)(2,1)}), bf16[512,1024]{1,0:T(8,128)(2,1)}) %all-gather.5.cloned.1.call-update) | async-done | bytes 1048592 | tf_op jit(solution)/shard_map/all_gather | solution.py:77
  94.9 1.5 %multiply_reduce_fusion = f32[1024]{0:T(1024)S(1)} fusion(bf16[512,1024]{1,0:T(8,128)(2,1)} %all-gather.5.cloned.1.call-done), kind=kLoop, calls=%fused_computation.6 | loop fusion | flops 1571840 | bytes 1052672 | tf_op jit(solution)/shard_map/reduce_sum | solution.py:80
  96.4 1.8 %reshape.109 = bf16[512,2,512]{2,1,0:T(2,128)(2,1)S(1)} reshape(bf16[512,1024]{1,0:T(8,128)(2,1)} %all-gather.5.cloned.1.call-done) | data formatting | bytes 2097152 | tf_op jit(solution)/shard_map/reshape | solution.py:78
  98.3 0.2 constant_dynamic-slice_fusion
  98.5 0.1 reduce_sum.38
  98.6 0.1 multiply_convert_fusion.3
  98.7 0.7 copy.47
  99.4 5.5 %all-to-all-start.2 = ((bf16[8,64,2,128]{3,1,2,0:T(8,128)(2,1)}), bf16[8,64,2,128]{3,1,2,0:T(8,128)(2,1)S(1)}, u32[]{:S(2)}, u32[]{:S(2)}) async-start(bf16[8,64,2,128]{3,1,2,0:T(8,128)(2,1)} %copy.47), calls=%async_computation.2 | async-start | bytes 524288 | tf_op jit(solution)/shard_map/all_to_all | solution.py:85
  105.0 0.1 copy.48
  105.0 0.1 reshape.111
  105.1 0.6 scatter_custom_fusion
  105.8 1.0 copy.49
  106.8 7.5 %all-to-all-done.2 = bf16[8,64,2,128]{3,1,2,0:T(8,128)(2,1)S(1)} async-done(((bf16[8,64,2,128]{3,1,2,0:T(8,128)(2,1)}), bf16[8,64,2,128]{3,1,2,0:T(8,128)(2,1)S(1)}, u32[]{:S(2)}, u32[]{:S(2)}) %all-to-all-start.2) | async-done | bytes 262176 | tf_op jit(solution)/shard_map/all_to_all | solution.py:85
  114.3 1.3 %gather_fusion.1 = bf16[16,64,128]{2,1,0:T(8,128)(2,1)} fusion(bf16[8,64,2,128]{3,1,2,0:T(8,128)(2,1)S(1)} %all-to-all-done.2, s32[16]{0:T(128)S(1)} %fusion.19), kind=kCustom, calls=%fused_computation.1 | custom fusion | bytes 524416 | tf_op jit(solution)/shard_map/gather | solution.py:94
  (23 shorter events, 0.2 us)
Async XLA Ops:
  7.2 1.8 %copy-start = (bf16[16,64,128]{2,1,0:T(8,128)(2,1)S(1)}, bf16[16,64,128]{2,1,0:T(8,128)(2,1)}, u32[]{:S(2)}) copy-start(bf16[16,64,128]{2,1,0:T(8,128)(2,1)} %param.4) | copy-start | bytes 786436
  7.2 35.2 %all-gather.3.cloned.1.call-start = ((), (), s32[]{:S(2)}) async-start(), calls=%async_computation.3 | async-start | bytes 1310720 | tf_op jit(solution)/shard_map/all_gather | solution.py:57
  26.4 18.3 %copy-start.5 = (f32[2,2,128,512]{3,2,1,0:T(8,128)S(1)}, f32[2,2,128,512]{3,2,1,0:T(8,128)}, u32[]{:S(2)}) copy-start(f32[2,2,128,512]{3,2,1,0:T(8,128)} %param.5) | copy-start | bytes 3145732
  42.4 1.8 %copy-start.1 = (bf16[2,512,512]{2,1,0:T(8,128)(2,1)S(1)}, bf16[2,512,512]{2,1,0:T(8,128)(2,1)}, u32[]{:S(2)}) copy-start(bf16[2,512,512]{2,1,0:T(8,128)(2,1)} %all-gather.3.cloned.1.call-done) | copy-start | bytes 3145732
  42.4 2.3 %copy-start.6 = (f32[128,512]{1,0:T(8,128)S(1)}, f32[128,512]{1,0:T(8,128)}, u32[]{:S(2)}) copy-start(f32[128,512]{1,0:T(8,128)} %fusion.12) | copy-start | bytes 786436
  46.1 17.9 %all-to-all-start.1 = ((bf16[4,2,128,512]{3,2,1,0:T(8,128)(2,1)}), bf16[4,2,128,512]{3,2,1,0:T(8,128)(2,1)S(1)}, u32[]{:S(2)}, u32[]{:S(2)}) async-start(bf16[4,2,128,512]{3,2,1,0:T(8,128)(2,1)} %bitcast.6), calls=%async_computation.1 | async-start | bytes 2097152 | tf_op jit(solution)/shard_map/all_to_all | solution.py:67
  49.6 45.3 %all-gather.5.cloned.1.call-start = ((), (), s32[]{:S(2)}) async-start(), calls=%async_computation.4 | async-start | bytes 1310720 | tf_op jit(solution)/shard_map/all_gather | solution.py:77
  64.5 1.7 %copy-start.2 = (f32[512,512]{1,0:T(8,128)S(1)}, f32[512,512]{1,0:T(8,128)}, u32[]{:S(2)}) copy-start(f32[512,512]{1,0:T(8,128)} %fusion.2) | copy-start | bytes 3145732
  65.2 1.0 copy-start.4
  66.2 1.7 %copy-start.3 = (f32[512,512]{1,0:T(8,128)S(1)}, f32[512,512]{1,0:T(8,128)}, u32[]{:S(2)}) copy-start(f32[512,512]{1,0:T(8,128)} %fusion.2) | copy-start | bytes 3145732
  74.4 1.0 copy-start.7
  99.4 14.8 %all-to-all-start.2 = ((bf16[8,64,2,128]{3,1,2,0:T(8,128)(2,1)}), bf16[8,64,2,128]{3,1,2,0:T(8,128)(2,1)S(1)}, u32[]{:S(2)}, u32[]{:S(2)}) async-start(bf16[8,64,2,128]{3,1,2,0:T(8,128)(2,1)} %copy.47), calls=%async_computation.2 | async-start | bytes 524288 | tf_op jit(solution)/shard_map/all_to_all | solution.py:85
Sparse Core Ops, SparseCore 0:
  26.5 15.8 all-gather.2
  78.1 16.8 all-gather.4
where the time goes:
time: 123 us; the launch traced here: 122 us
  waiting for transfers between devices  52.4 us (43%)
  blocking collectives  16 us (13%)
  between operations  15 us (12%)
  matrix products  12.9 us (10%)
  local copies, waits for them, and re-layouts  10.6 us (9%)
  starting transfers between devices  9.11 us (7%)
  other arithmetic  6.43 us (5%)
    all_gather x1, waiting for transfers between devices, body(): all_parts = lax.all_gather(result, 'mp', axis=1, tiled=True)  16.6 us
    all_to_all x1, blocking collectives, body(): lax.all_to_all(outgoing, 'dp', split_axis=1, concat_axis=1, tiled=True)  16 us
    all_gather x1, waiting for transfers between devices, body(): blocks = lax.all_gather(col_part, 'mp', axis=2, tiled=True)  15.2 us
    all_to_all x1, waiting for transfers between devices, body(): lax.all_to_all(spread_rows, 'mp', split_axis=0, concat_axis=2, tiled=True)  13.2 us
    all_to_all x1, waiting for transfers between devices, body(): lax.all_to_all(outgoing_back, 'dp', split_axis=0, concat_axis=0, tiled=True)  7.46 us
    all_to_all x1, starting transfers between devices, body(): lax.all_to_all(outgoing_back, 'dp', split_axis=0, concat_axis=0, tiled=True)  5.51 us
    dot_general x1, matrix products, newton_root(): jnp.einsum('sij,sjk->sik', square, partial_m, preferred_element_type=jnp....  4.21 us
    all_to_all x1, starting transfers between devices, body(): lax.all_to_all(spread_rows, 'mp', split_axis=0, concat_axis=2, tiled=True)  3.52 us
  transfers between devices with their start and end apart: 4, of which 4 were waited for; matrix products, arithmetic and copies ran while one was open for 3% of the time, Pallas kernels for 0%

commit v1 on v0

--- a/solution.py
+++ b/solution.py
@@ -52,7 +52,24 @@
     my_part = my_index % per_slot
     owners = jnp.roll(owner_blocks, rotation[0], axis=0)
     outgoing = jnp.take(grad_tiles, owners.T, axis=0)
-    arrived = lax.all_to_all(outgoing, "dp", split_axis=1, concat_axis=1, tiled=True)
+    w1 = lax.axis_index("dp")
+    response = lax.axis_size("dp")
+    step_out, shaped = (response, w1)
+    g_now = outgoing.shape[1] // step_out
+    answer = list(outgoing.shape)
+    answer[1] = g_now
+    extra = answer[1]
+    answer[1] = extra * step_out
+    u = 0
+    arrived = jnp.zeros(answer, outgoing.dtype)
+    while u < step_out:
+        f_next = lax.dynamic_slice_in_dim(outgoing, (shaped ^ u) * g_now, g_now, axis=1)
+        if u:
+            f_next = lax.ppermute(
+                f_next, axis_name="dp", perm=[(dev, dev ^ u) for dev in range(step_out)]
+            )
+        arrived = lax.dynamic_update_slice_in_dim(arrived, f_next, (shaped ^ u) * extra, axis=1)
+        u = u + 1
     col_part = arrived.reshape(slots, order, tile_cols)
     blocks = lax.all_gather(col_part, "mp", axis=2, tiled=True)
     row_part = lax.dynamic_slice_in_dim(blocks, my_index * rows_each, rows_each, 1)

time: 123 us -> 124 us (level)
  blocking collectives: 16 us -> 0 us
  starting transfers between devices: 9.11 us -> 21.7 us
  waiting for transfers between devices: 52.4 us -> 57.2 us
    all_to_all x1 -> x0, blocking collectives: 16 us -> none  [body(): lax.all_to_all(outgoing, 'dp', split_axis=1, concat_axis=1, tiled=True)]
    ppermute x0 -> x7, starting transfers between devices: none -> 12.6 us  [body(): lax.ppermute(f_next, axis_name='dp', perm=[(dev, dev ^ u) for dev in rang...]
    ppermute x0 -> x7, waiting for transfers between devices: none -> 6.49 us  [body(): lax.ppermute(f_next, axis_name='dp', perm=[(dev, dev ^ u) for dev in rang...]
    all_gather x1, waiting for transfers between devices: 15.2 us -> 13.5 us  [body(): blocks = lax.all_gather(col_part, 'mp', axis=2, tiled=True)]
    unnamed x17 -> x19, local copies, waits for them, and re-layouts: 3 us -> 3.71 us
  transfers between devices with their start and end apart: 4 -> 11, of which waited for: 4 -> 7; matrix products, arithmetic and copies ran while one was open for 3% -> 3% of each run, Pallas kernels for 0% -> 0%
where the time goes in v1:
time: 124 us
  waiting for transfers between devices  57.2 us (46%)
  starting transfers between devices  21.7 us (18%)
  between operations  15.1 us (12%)
  matrix products  12.8 us (10%)
  local copies, waits for them, and re-layouts  10.7 us (9%)
  other arithmetic  6.38 us (5%)
    all_gather x1, waiting for transfers between devices, body(): all_parts = lax.all_gather(result, 'mp', axis=1, tiled=True)  16.6 us
    all_gather x1, waiting for transfers between devices, body(): blocks = lax.all_gather(col_part, 'mp', axis=2, tiled=True)  13.5 us
    all_to_all x1, waiting for transfers between devices, body(): lax.all_to_all(spread_rows, 'mp', split_axis=0, concat_axis=2, tiled=True)  13.2 us
    ppermute x7, starting transfers between devices, body(): lax.ppermute(f_next, axis_name='dp', perm=[(dev, dev ^ u) for dev in rang...  12.6 us
    all_to_all x1, waiting for transfers between devices, body(): lax.all_to_all(outgoing_back, 'dp', split_axis=0, concat_axis=0, tiled=True)  7.46 us
    ppermute x7, waiting for transfers between devices, body(): lax.ppermute(f_next, axis_name='dp', perm=[(dev, dev ^ u) for dev in rang...  6.49 us
    all_to_all x1, starting transfers between devices, body(): lax.all_to_all(outgoing_back, 'dp', split_axis=0, concat_axis=0, tiled=True)  5.51 us
    dot_general x1, matrix products, newton_root(): jnp.einsum('sij,sjk->sik', square, partial_m, preferred_element_type=jnp....  4.15 us
  transfers between devices with their start and end apart: 11, of which 7 were waited for; matrix products, arithmetic and copies ran while one was open for 3% of the time, Pallas kernels for 0%

profile of v1, /device:TPU:0, one launch (start us, length us, event | category | flops | bytes accessed | tf_op | source)
XLA Modules:
  0.0 123.9 jit_solution(9680982481323596238)
XLA Ops:
  8.0 0.8 pad_add_fusion
  8.8 0.1 compare_and_fusion
  8.9 0.1 reshape.116
  9.0 0.6 gather_fusion
  9.6 0.1 broadcast_select_fusion
  9.8 3.0 %collective-permute-start = (bf16[2,1,64,128]{3,2,1,0:T(8,128)(2,1)S(1)}, bf16[2,1,64,128]{3,2,1,0:T(8,128)(2,1)S(1)}, u32[]{:S(2)}, u32[]{:S(2)}) collective-permute-start(bf16[2,1,64,128]{3,2,1,0:T(8,128)(2,1)S(1)} %get-tuple-element.22), channel_id=1, source_target_pairs={{0,4},{4,0},{8,12},{12,8},{16,20},{20,16},{24,28},{28,24},{1,5},{5... | collective-permute-start | bytes 98312 | tf_op jit(solution)/shard_map/ppermute | solution.py:68
  12.8 1.6 %collective-permute-start.1 = (bf16[2,1,64,128]{3,2,1,0:T(8,128)(2,1)S(1)}, bf16[2,1,64,128]{3,2,1,0:T(8,128)(2,1)S(1)}, u32[]{:S(2)}, u32[]{:S(2)}) collective-permute-start(bf16[2,1,64,128]{3,2,1,0:T(8,128)(2,1)S(1)} %get-tuple-element.21), channel_id=1, source_target_pairs={{0,8},{4,12},{8,0},{12,4},{16,24},{20,28},{24,16},{28,20},{1,9},{5... | collective-permute-start | bytes 98312 | tf_op jit(solution)/shard_map/ppermute | solution.py:68
  14.4 3.0 %collective-permute-start.3 = (bf16[2,1,64,128]{3,2,1,0:T(8,128)(2,1)S(1)}, bf16[2,1,64,128]{3,2,1,0:T(8,128)(2,1)S(1)}, u32[]{:S(2)}, u32[]{:S(2)}) collective-permute-start(bf16[2,1,64,128]{3,2,1,0:T(8,128)(2,1)S(1)} %get-tuple-element.19), channel_id=1, source_target_pairs={{0,16},{4,20},{8,24},{12,28},{16,0},{20,4},{24,8},{28,12},{1,17},{... | collective-permute-start | bytes 98312 | tf_op jit(solution)/shard_map/ppermute | solution.py:68
  17.4 1.3 %collective-permute-start.4 = (bf16[2,1,64,128]{3,2,1,0:T(8,128)(2,1)S(1)}, bf16[2,1,64,128]{3,2,1,0:T(8,128)(2,1)S(1)}, u32[]{:S(2)}, u32[]{:S(2)}) collective-permute-start(bf16[2,1,64,128]{3,2,1,0:T(8,128)(2,1)S(1)} %get-tuple-element.18), channel_id=1, source_target_pairs={{0,20},{4,16},{8,28},{12,24},{16,4},{20,0},{24,12},{28,8},{1,21},{... | collective-permute-start | bytes 98312 | tf_op jit(solution)/shard_map/ppermute | solution.py:68
  18.7 3.6 %collective-permute-start.5 = (bf16[2,1,64,128]{3,2,1,0:T(8,128)(2,1)S(1)}, bf16[2,1,64,128]{3,2,1,0:T(8,128)(2,1)S(1)}, u32[]{:S(2)}, u32[]{:S(2)}) collective-permute-start(bf16[2,1,64,128]{3,2,1,0:T(8,128)(2,1)S(1)} %get-tuple-element.17), channel_id=1, source_target_pairs={{0,24},{4,28},{8,16},{12,20},{16,8},{20,12},{24,0},{28,4},{1,25},{... | collective-permute-start | bytes 98312 | tf_op jit(solution)/shard_map/ppermute | solution.py:68
  22.5 0.8 collective-permute-done.4
  23.3 1.3 %collective-permute-done.5 = bf16[2,1,64,128]{3,2,1,0:T(8,128)(2,1)S(1)} collective-permute-done((bf16[2,1,64,128]{3,2,1,0:T(8,128)(2,1)S(1)}, bf16[2,1,64,128]{3,2,1,0:T(8,128)(2,1)S(1)}, u32[]{:S(2)}, u32[]{:S(2)}) %collective-permute-start.5) | collective-permute-done | bytes 32800 | tf_op jit(solution)/shard_map/ppermute | solution.py:68
  24.5 4.4 %collective-permute-done.6 = bf16[2,1,64,128]{3,2,1,0:T(8,128)(2,1)S(1)} collective-permute-done((bf16[2,1,64,128]{3,2,1,0:T(8,128)(2,1)S(1)}, bf16[2,1,64,128]{3,2,1,0:T(8,128)(2,1)S(1)}, u32[]{:S(2)}, u32[]{:S(2)}) %collective-permute-start.6) | collective-permute-done | bytes 32800 | tf_op jit(solution)/shard_map/ppermute | solution.py:68
  29.0 0.7 copy-done.2
  29.7 0.8 fusion.12
  30.5 13.5 %all-gather.3.cloned.1.call-done = bf16[2,512,512]{2,1,0:T(8,128)(2,1)} async-done(((bf16[2,512,128]{2,1,0:T(8,128)(2,1)}), bf16[2,512,512]{2,1,0:T(8,128)(2,1)}) %all-gather.3.cloned.1.call-update) | async-done | bytes 1048592 | tf_op jit(solution)/shard_map/all_gather | solution.py:74
  44.0 1.7 %convolution_bitcast_fusion = f32[2,1,128,512]{3,2,0,1:T(8,128)S(1)} fusion(bf16[2,512,128]{2,1,0:T(8,128)(2,1)} %bitcast.43, bf16[2,512,512]{2,1,0:T(8,128)(2,1)} %all-gather.3.cloned.1.call-done), kind=kOutput, calls=%fused_computation.15 | convolution fusion | flops 134217728 | bytes 1835008 | tf_op jit(solution)/shard_map/kji,kjl->kil/dot_general | solution.py:77
  45.8 0.5 convolution_bitcast_fusion.1
  46.3 0.3 add_convert_fusion
  46.6 1.1 broadcast_in_dim.36
  47.7 3.5 %all-to-all-start = ((bf16[4,2,128,512]{3,2,1,0:T(8,128)(2,1)}), bf16[4,2,128,512]{3,2,1,0:T(8,128)(2,1)S(1)}, u32[]{:S(2)}, u32[]{:S(2)}) async-start(bf16[4,2,128,512]{3,2,1,0:T(8,128)(2,1)} %bitcast.6), calls=%async_computation | async-start | bytes 2097152 | tf_op jit(solution)/shard_map/all_to_all | solution.py:84
  51.3 1.1 fusion.2
  52.4 13.2 %all-to-all-done = bf16[4,2,128,512]{3,2,1,0:T(8,128)(2,1)S(1)} async-done(((bf16[4,2,128,512]{3,2,1,0:T(8,128)(2,1)}), bf16[4,2,128,512]{3,2,1,0:T(8,128)(2,1)S(1)}, u32[]{:S(2)}, u32[]{:S(2)}) %all-to-all-start) | async-done | bytes 1048608 | tf_op jit(solution)/shard_map/all_to_all | solution.py:84
  65.6 0.3 convert_bitcast_fusion
  65.9 0.2 copy.31
  66.1 0.4 fusion
  66.5 0.3 multiply_convert_fusion.2
  66.8 1.0 copy-done.5
  67.8 1.7 %convolution_convert_fusion.3 = bf16[2,512,512]{2,1,0:T(8,128)(2,1)} fusion(bf16[2,512,512]{2,1,0:T(8,128)(2,1)S(1)} %multiply_convert_fusion.2, f32[512,512]{1,0:T(8,128)S(1)} %copy-done.3), kind=kOutput, calls=%fused_computation.14 | convolution fusion | flops 539492352 | bytes 3145728 | tf_op jit(solution)/shard_map/sij,sjk->sik/dot_general | solution.py:27
  69.5 4.2 %multiply_convert_fusion = bf16[2,512,512]{2,1,0:T(8,128)(2,1)} fusion(bf16[2,512,512]{2,1,0:T(8,128)(2,1)} %convolution_convert_fusion.3, bf16[2,512,512]{2,1,0:T(8,128)(2,1)} %copy-done.5, f32[512,512]{1,0:T(8,128)S(1)} %copy-done.4), kind=kOutput, calls=%fused_computation.8 | convolution fusion | flops 1076887552 | bytes 4194304 | tf_op jit(solution)/shard_map/sij,sjk->sik/dot_general | solution.py:33
  73.7 2.3 %convolution_convert_fusion = bf16[2,512,512]{2,1,0:T(8,128)(2,1)S(1)} fusion(bf16[2,512,512]{2,1,0:T(8,128)(2,1)} %multiply_convert_fusion, bf16[2,512,512]{2,1,0:T(8,128)(2,1)} %copy-done.5, f32[512,512]{1,0:T(8,128)S(1)} %copy-done.4), kind=kOutput, calls=%fused_computation.11 | convolution fusion | flops 539492352 | bytes 4194304 | tf_op jit(solution)/shard_map/sij,sjk->sik/dot_general | solution.py:23
  76.0 1.0 copy-done.8
  77.0 2.5 %convolution_convert_fusion.4 = bf16[512,256]{1,0:T(8,128)(2,1)} fusion(bf16[2,512,512]{2,1,0:T(8,128)(2,1)} %copy-done.8, bf16[2,512,512]{2,1,0:T(8,128)(2,1)S(1)} %copy-done.1, s32[]{:T(128)S(6)} %select_n.116, bf16[1,512,512]{2,1,0:T(8,128)(2,1)S(1)} %slice.13, s32[]{:T(128)S(6)} %select_n.118), kind=kOutput, calls=%fused_computation.17 | convolution fusion | flops 268697600 | bytes 1572872 | tf_op jit(solution)/shard_map/dot_general | solution.py:91
  79.5 0.4 multiply_reduce_fusion.1
  79.9 16.6 %all-gather.5.cloned.1.call-done = bf16[512,1024]{1,0:T(8,128)(2,1)} async-done(((bf16[512,256]{1,0:T(8,128)(2,1)}), bf16[512,1024]{1,0:T(8,128)(2,1)}) %all-gather.5.cloned.1.call-update) | async-done | bytes 1048592 | tf_op jit(solution)/shard_map/all_gather | solution.py:94
  96.4 1.5 %multiply_reduce_fusion = f32[1024]{0:T(1024)S(1)} fusion(bf16[512,1024]{1,0:T(8,128)(2,1)} %all-gather.5.cloned.1.call-done), kind=kLoop, calls=%fused_computation.6 | loop fusion | flops 1571840 | bytes 1052672 | tf_op jit(solution)/shard_map/reduce_sum | solution.py:97
  97.9 1.8 %reshape.109 = bf16[512,2,512]{2,1,0:T(2,128)(2,1)S(1)} reshape(bf16[512,1024]{1,0:T(8,128)(2,1)} %all-gather.5.cloned.1.call-done) | data formatting | bytes 2097152 | tf_op jit(solution)/shard_map/reshape | solution.py:95
  99.8 0.2 constant_dynamic-slice_fusion
  100.0 0.1 reduce_sum.38
  100.1 0.1 multiply_convert_fusion.3
  100.2 0.7 copy.33
  101.0 5.5 %all-to-all-start.1 = ((bf16[8,64,2,128]{3,1,2,0:T(8,128)(2,1)}), bf16[8,64,2,128]{3,1,2,0:T(8,128)(2,1)S(1)}, u32[]{:S(2)}, u32[]{:S(2)}) async-start(bf16[8,64,2,128]{3,1,2,0:T(8,128)(2,1)} %copy.33), calls=%async_computation.1 | async-start | bytes 524288 | tf_op jit(solution)/shard_map/all_to_all | solution.py:102
  106.5 0.1 copy.34
  106.6 0.1 reshape.111
  106.6 0.6 scatter_custom_fusion
  107.3 1.0 copy.35
  108.3 7.5 %all-to-all-done.1 = bf16[8,64,2,128]{3,1,2,0:T(8,128)(2,1)S(1)} async-done(((bf16[8,64,2,128]{3,1,2,0:T(8,128)(2,1)}), bf16[8,64,2,128]{3,1,2,0:T(8,128)(2,1)S(1)}, u32[]{:S(2)}, u32[]{:S(2)}) %all-to-all-start.1) | async-done | bytes 262176 | tf_op jit(solution)/shard_map/all_to_all | solution.py:102
  115.8 1.3 %gather_fusion.1 = bf16[16,64,128]{2,1,0:T(8,128)(2,1)} fusion(bf16[8,64,2,128]{3,1,2,0:T(8,128)(2,1)S(1)} %all-to-all-done.1, s32[16]{0:T(128)S(1)} %fusion.19), kind=kCustom, calls=%fused_computation.1 | custom fusion | bytes 524416 | tf_op jit(solution)/shard_map/gather | solution.py:111
  (45 shorter events, 0.5 us)
Async XLA Ops:
  7.2 1.8 %copy-start = (bf16[16,64,128]{2,1,0:T(8,128)(2,1)S(1)}, bf16[16,64,128]{2,1,0:T(8,128)(2,1)}, u32[]{:S(2)}) copy-start(bf16[16,64,128]{2,1,0:T(8,128)(2,1)} %param.4) | copy-start | bytes 786436
  7.2 36.8 %all-gather.3.cloned.1.call-start = ((), (), s32[]{:S(2)}) async-start(), calls=%async_computation.2 | async-start | bytes 1310720 | tf_op jit(solution)/shard_map/all_gather | solution.py:74
  9.8 8.9 %collective-permute-start = (bf16[2,1,64,128]{3,2,1,0:T(8,128)(2,1)S(1)}, bf16[2,1,64,128]{3,2,1,0:T(8,128)(2,1)S(1)}, u32[]{:S(2)}, u32[]{:S(2)}) collective-permute-start(bf16[2,1,64,128]{3,2,1,0:T(8,128)(2,1)S(1)} %get-tuple-element.22), channel_id=1, source_target_pairs={{0,4},{4,0},{8,12},{12,8},{16,20},{20,16},{24,28},{28,24},{1,5},{5... | collective-permute-start | bytes 98312 | tf_op jit(solution)/shard_map/ppermute | solution.py:68
  12.8 9.5 %collective-permute-start.1 = (bf16[2,1,64,128]{3,2,1,0:T(8,128)(2,1)S(1)}, bf16[2,1,64,128]{3,2,1,0:T(8,128)(2,1)S(1)}, u32[]{:S(2)}, u32[]{:S(2)}) collective-permute-start(bf16[2,1,64,128]{3,2,1,0:T(8,128)(2,1)S(1)} %get-tuple-element.21), channel_id=1, source_target_pairs={{0,8},{4,12},{8,0},{12,4},{16,24},{20,28},{24,16},{28,20},{1,9},{5... | collective-permute-start | bytes 98312 | tf_op jit(solution)/shard_map/ppermute | solution.py:68
  14.4 8.0 %collective-permute-start.2 = (bf16[2,1,64,128]{3,2,1,0:T(8,128)(2,1)S(1)}, bf16[2,1,64,128]{3,2,1,0:T(8,128)(2,1)S(1)}, u32[]{:S(2)}, u32[]{:S(2)}) collective-permute-start(bf16[2,1,64,128]{3,2,1,0:T(8,128)(2,1)S(1)} %get-tuple-element.20), channel_id=1, source_target_pairs={{0,12},{4,8},{8,4},{12,0},{16,28},{20,24},{24,20},{28,16},{1,13},{... | collective-permute-start | bytes 98312 | tf_op jit(solution)/shard_map/ppermute | solution.py:68
  14.4 8.0 %collective-permute-start.3 = (bf16[2,1,64,128]{3,2,1,0:T(8,128)(2,1)S(1)}, bf16[2,1,64,128]{3,2,1,0:T(8,128)(2,1)S(1)}, u32[]{:S(2)}, u32[]{:S(2)}) collective-permute-start(bf16[2,1,64,128]{3,2,1,0:T(8,128)(2,1)S(1)} %get-tuple-element.19), channel_id=1, source_target_pairs={{0,16},{4,20},{8,24},{12,28},{16,0},{20,4},{24,8},{28,12},{1,17},{... | collective-permute-start | bytes 98312 | tf_op jit(solution)/shard_map/ppermute | solution.py:68
  17.4 5.8 %collective-permute-start.4 = (bf16[2,1,64,128]{3,2,1,0:T(8,128)(2,1)S(1)}, bf16[2,1,64,128]{3,2,1,0:T(8,128)(2,1)S(1)}, u32[]{:S(2)}, u32[]{:S(2)}) collective-permute-start(bf16[2,1,64,128]{3,2,1,0:T(8,128)(2,1)S(1)} %get-tuple-element.18), channel_id=1, source_target_pairs={{0,20},{4,16},{8,28},{12,24},{16,4},{20,0},{24,12},{28,8},{1,21},{... | collective-permute-start | bytes 98312 | tf_op jit(solution)/shard_map/ppermute | solution.py:68
  18.7 5.8 %collective-permute-start.5 = (bf16[2,1,64,128]{3,2,1,0:T(8,128)(2,1)S(1)}, bf16[2,1,64,128]{3,2,1,0:T(8,128)(2,1)S(1)}, u32[]{:S(2)}, u32[]{:S(2)}) collective-permute-start(bf16[2,1,64,128]{3,2,1,0:T(8,128)(2,1)S(1)} %get-tuple-element.17), channel_id=1, source_target_pairs={{0,24},{4,28},{8,16},{12,20},{16,8},{20,12},{24,0},{28,4},{1,25},{... | collective-permute-start | bytes 98312 | tf_op jit(solution)/shard_map/ppermute | solution.py:68
  22.3 6.7 %collective-permute-start.6 = (bf16[2,1,64,128]{3,2,1,0:T(8,128)(2,1)S(1)}, bf16[2,1,64,128]{3,2,1,0:T(8,128)(2,1)S(1)}, u32[]{:S(2)}, u32[]{:S(2)}) collective-permute-start(bf16[2,1,64,128]{3,2,1,0:T(8,128)(2,1)S(1)} %get-tuple-element.16), channel_id=1, source_target_pairs={{0,28},{4,24},{8,20},{12,16},{16,12},{20,8},{24,4},{28,0},{1,29},{... | collective-permute-start | bytes 98312 | tf_op jit(solution)/shard_map/ppermute | solution.py:68
  22.4 23.8 %copy-start.6 = (f32[2,2,128,512]{3,2,1,0:T(8,128)S(1)}, f32[2,2,128,512]{3,2,1,0:T(8,128)}, u32[]{:S(2)}) copy-start(f32[2,2,128,512]{3,2,1,0:T(8,128)} %param.5) | copy-start | bytes 3145732
  29.0 0.7 copy-start.2
  44.0 1.8 %copy-start.1 = (bf16[2,512,512]{2,1,0:T(8,128)(2,1)S(1)}, bf16[2,512,512]{2,1,0:T(8,128)(2,1)}, u32[]{:S(2)}) copy-start(bf16[2,512,512]{2,1,0:T(8,128)(2,1)} %all-gather.3.cloned.1.call-done) | copy-start | bytes 3145732
  44.0 2.3 %copy-start.7 = (f32[128,512]{1,0:T(8,128)S(1)}, f32[128,512]{1,0:T(8,128)}, u32[]{:S(2)}) copy-start(f32[128,512]{1,0:T(8,128)} %fusion.12) | copy-start | bytes 786436
  47.7 17.9 %all-to-all-start = ((bf16[4,2,128,512]{3,2,1,0:T(8,128)(2,1)}), bf16[4,2,128,512]{3,2,1,0:T(8,128)(2,1)S(1)}, u32[]{:S(2)}, u32[]{:S(2)}) async-start(bf16[4,2,128,512]{3,2,1,0:T(8,128)(2,1)} %bitcast.6), calls=%async_computation | async-start | bytes 2097152 | tf_op jit(solution)/shard_map/all_to_all | solution.py:84
  51.2 45.2 %all-gather.5.cloned.1.call-start = ((), (), s32[]{:S(2)}) async-start(), calls=%async_computation.3 | async-start | bytes 1310720 | tf_op jit(solution)/shard_map/all_gather | solution.py:94
  66.1 1.7 %copy-start.3 = (f32[512,512]{1,0:T(8,128)S(1)}, f32[512,512]{1,0:T(8,128)}, u32[]{:S(2)}) copy-start(f32[512,512]{1,0:T(8,128)} %fusion.2) | copy-start | bytes 3145732
  66.8 1.0 copy-start.5
  67.8 1.7 %copy-start.4 = (f32[512,512]{1,0:T(8,128)S(1)}, f32[512,512]{1,0:T(8,128)}, u32[]{:S(2)}) copy-start(f32[512,512]{1,0:T(8,128)} %fusion.2) | copy-start | bytes 3145732
  75.9 1.0 copy-start.8
  101.0 14.8 %all-to-all-start.1 = ((bf16[8,64,2,128]{3,1,2,0:T(8,128)(2,1)}), bf16[8,64,2,128]{3,1,2,0:T(8,128)(2,1)S(1)}, u32[]{:S(2)}, u32[]{:S(2)}) async-start(bf16[8,64,2,128]{3,1,2,0:T(8,128)(2,1)} %copy.33), calls=%async_computation.1 | async-start | bytes 524288 | tf_op jit(solution)/shard_map/all_to_all | solution.py:102
Sparse Core Ops, SparseCore 0:
  29.8 14.0 all-gather.2
  79.6 16.8 all-gather.4
